TPU v7x, 32 devices: a whole 2x2x4 slice. The times are simulated.
32 devices in a mesh: wide: 8 (over y, x, core), narrow: 4 (over z).
Axes of the slice: x: 2, y: 2, z: 4, core: 2. Of those that a mesh axis runs over, the one named last changes fastest.
Arguments:
- first_state: float32 [2, 32768, 1024], P(None, ('wide', 'narrow')), may hold values from -100 to 100
- second_state: float32 [2, 32768, 1024], P(None, ('wide', 'narrow')), may hold values from -200 to 200
- place_first: int32 [32768], replicated, may hold values from 0 to 32767, as said below
- place_second: int32 [32768], replicated, may hold values from 0 to 32767, as said below
Outputs:
- aligned: float32 [2, 32768, 1024], P(None, ('wide', 'narrow'))
- intersection: float32 [2], replicated
- norms: float32 [2], replicated
Inputs may be any that keep to these rules, and one draw needn't show every extreme that they name: Each of place_first and place_second maps a logical block index to a storage block index by a permutation of the index's bits. Every logical bit that selects a device (the high bits of a storage index above its position within a device) in one state's order selects a block within a device in the other's, so each device holds exactly 32 blocks of the second state that the first state's order places on any given device. `place_second`: drawn together with place_first under the rule stated there.
All inputs are finite; a program needn't handle non-finite values.
Results may differ from a plain program's by a relative error of at most 0.00002.
Values sent between devices are 32-bit elements; how exact they have to be, the bound alone decides.
A program may use at most 128 MiB of HBM per device.

v0:
```python
import functools

import jax
import jax.numpy as jnp
from jax import lax
from jax.experimental import pallas as pl
from jax.experimental.pallas import tpu as pltpu
from jax.sharding import PartitionSpec as P

MESH = pl.DeviceIdType.MESH
SUB = 8
LANE = 128


def row_weight(one_hot):
    return jnp.where(one_hot < SUB, one_hot, one_hot * SUB)


def bits(count):
    return count.bit_length() - 1


def table(ref, base, weights, start=0):
    ref[base] = jnp.int32(start)
    for level, weight in enumerate(weights):
        for low in range(1 << level):
            ref[base + (1 << level) + low] = ref[base + low] + weight


def build_tables(place_f, place_s, blocks_dev, devices, me, share, rows_out, rows_in, back):
    levels = bits(blocks_dev * devices)
    zero = jnp.int32(0)
    dev_out = [zero] * bits(devices)
    dev_in = [zero] * bits(devices)
    k_out = [zero] * bits(share)
    k_in = [zero] * bits(share)
    slot_back = [zero] * bits(blocks_dev)
    unit = jnp.int32(1)
    for level in range(levels):
        f = place_f(level)
        s = place_s(level)
        f_dev = f >> bits(blocks_dev)
        s_dev = s >> bits(blocks_dev)
        both = (f_dev == 0) & (s_dev == 0)
        for j in range(bits(devices)):
            dev_out[j] = dev_out[j] + jnp.where(f_dev == (1 << j), row_weight(s), 0)
            dev_in[j] = dev_in[j] + jnp.where(s_dev == (1 << j), row_weight(f), 0)
        for i in range(bits(share)):
            here = both & (unit == (1 << i))
            k_out[i] = k_out[i] + jnp.where(here, row_weight(s), 0)
            k_in[i] = k_in[i] + jnp.where(here, row_weight(f), 0)
        toward = jnp.where((s_dev & me) == 0, s_dev, -s_dev)
        packed = jnp.where(both, unit * SUB, toward * (2 * share * SUB))
        for p in range(bits(blocks_dev)):
            slot_back[p] = slot_back[p] + jnp.where(f == (1 << p), packed, 0)
        unit = jnp.where(both, unit * 2, unit)
    table(rows_out, 0, dev_out)
    table(rows_out, devices, k_out)
    table(rows_in, 0, dev_in)
    table(rows_in, devices, k_in)
    table(back, 0, slot_back[:bits(SUB)], me * (2 * share * SUB))
    table(back, SUB, slot_back[bits(SUB):])


def exchange(sizes, blocks_dev, share, pieces, amp_total, place_first, place_second, first_hbm, second_hbm,
             out_hbm, intersection, norms,
             first, second, outgoing, arrived, stats, totals, powers, rows_out, rows_in, back,
             load_sem, place_sem, send_sem, recv_sem, out_sem, sq_send, sq_recv, dot_send, dot_recv):
    wide_count, narrow_count = sizes
    devices = wide_count * narrow_count
    levels = bits(blocks_dev * devices)
    me_w = lax.axis_index("wide")
    me_n = lax.axis_index("narrow")
    me = me_w * narrow_count + me_n
    part_rows = blocks_dev * SUB
    message = 2 * share * SUB

    lines = [0] + [1 << line for line in range(levels - bits(LANE))]
    fetches = []
    for which, place in enumerate((place_first, place_second)):
        for at, line in enumerate(lines):
            fetches.append(pltpu.make_async_copy(
                place.at[pl.ds(line, 1), :], powers.at[which, pl.ds(at, 1), :],
                place_sem.at[which * len(lines) + at]))
    load_second = pltpu.make_async_copy(second_hbm, second, load_sem.at[0])
    load_first = pltpu.make_async_copy(first_hbm, first, load_sem.at[1])
    for fetch in fetches:
        fetch.start()
    load_second.start()

    def partner(offset):
        return (jnp.bitwise_xor(me_w, offset // narrow_count),
                jnp.bitwise_xor(me_n, lax.rem(offset, narrow_count)))

    def other(offset):
        other_w, other_n = partner(offset)
        return other_w * narrow_count + other_n

    barrier = pltpu.get_barrier_semaphore()

    @pl.loop(1, devices)
    def _(offset):
        pl.semaphore_signal(barrier, inc=1, device_id=partner(offset), device_id_type=MESH)

    for fetch in fetches:
        fetch.wait()

    def place_of(which):
        def entry(level):
            if (1 << level) < LANE:
                return powers[which, 0, 1 << level]
            return powers[which, 1 + level - bits(LANE), 0]
        return entry

    build_tables(place_of(0), place_of(1), blocks_dev, devices, me, share, rows_out, rows_in, back)
    load_second.wait()
    load_first.start()
    pl.semaphore_wait(barrier, devices - 1)

    last = narrow_count - 1
    inner = (me_n != 0) & (me_n != last)
    flip = jnp.where(lax.rem(me_w, 2) == 1, wide_count - 2, 0)

    def offset_of(seq):
        turn = seq // wide_count
        far = jnp.where(inner, jnp.where(turn == 0, last, turn), turn + 1)
        away = jnp.bitwise_xor(lax.rem(seq, wide_count), flip) * narrow_count + far
        near = (seq - wide_count * last + 1) * narrow_count
        return jnp.where(turn < last, away, near)

    outside = wide_count * last

    def rows_at(ref, offset):
        return ref.at[pl.ds(pl.multiple_of(offset * message, message), message), :]

    def block_at(offset, part, k):
        return pl.ds(pl.multiple_of(offset * message + (part * share + k) * SUB, SUB), SUB)

    def block_copy(offset):
        return pltpu.make_async_remote_copy(
            src_ref=rows_at(outgoing, offset), dst_ref=rows_at(arrived, offset),
            send_sem=send_sem.at[offset], recv_sem=recv_sem.at[offset],
            device_id=partner(offset), device_id_type=MESH)

    def pack(offset, out):
        base = rows_out[other(offset)]

        def row(k, carry):
            start = base + rows_out[devices + k]
            for part in range(2):
                out[block_at(offset, part, k), :] = second[pl.ds(start + part * part_rows, SUB, stride=SUB), :]
            return carry

        lax.fori_loop(0, share, row, 0, unroll=min(8, share))

    pack(offset_of(0), outgoing)

    @pl.loop(1, devices - 1)
    def _(seq):
        pack(offset_of(seq), outgoing)

        @pl.when(seq <= outside)
        def _():
            block_copy(offset_of(seq - 1)).start()

    pack(0, arrived)

    load_first.wait()
    chunk = 16 * SUB

    def squares(i, carry):
        at = pl.multiple_of(i * chunk, chunk)
        a = first[pl.ds(at, chunk), :].reshape(chunk // SUB, SUB, LANE)
        b = second[pl.ds(at, chunk), :].reshape(chunk // SUB, SUB, LANE)
        return carry[0] + jnp.sum(a * a, axis=0), carry[1] + jnp.sum(b * b, axis=0)

    zero = jnp.zeros((SUB, LANE), jnp.float32)
    sq_first, sq_second = lax.fori_loop(0, 2 * part_rows // chunk, squares, (zero, zero))
    stats[0, 0] = sq_first
    stats[0, 1] = sq_second

    def dots(offset, carry):
        base = rows_in[other(offset)]

        def row(k, carry):
            real, imag = carry
            start = base + rows_in[devices + k]
            f_re = first[pl.ds(start, SUB, stride=SUB), :]
            f_im = first[pl.ds(start + part_rows, SUB, stride=SUB), :]
            g_re = arrived[block_at(offset, 0, k), :]
            g_im = arrived[block_at(offset, 1, k), :]
            return real + (f_re * g_re + f_im * g_im), imag + (f_re * g_im - f_im * g_re)

        return lax.fori_loop(0, share, row, carry, unroll=min(8, share))

    carry = dots(0, (zero, zero))

    def sum_copy(kind, sems, offset):
        return pltpu.make_async_remote_copy(
            src_ref=stats.at[kind], dst_ref=totals.at[kind, offset],
            send_sem=sems[0].at[offset], recv_sem=sems[1].at[offset],
            device_id=partner(offset), device_id_type=MESH)

    sq_copy = functools.partial(sum_copy, 0, (sq_send, sq_recv))
    dot_copy = functools.partial(sum_copy, 1, (dot_send, dot_recv))

    @pl.loop(1, devices)
    def _(offset):
        sq_copy(offset).start()

    def take(offset, carry):
        block_copy(offset).wait_recv()
        return dots(offset, carry)

    def take_and_send(seq, carry):
        block_copy(offset_of(outside + seq)).start()
        return take(offset_of_arrival(seq), carry)

    def offset_of_arrival(seq):
        turn = seq // wide_count
        far = jnp.where(inner, jnp.where(turn == 0, last, turn), turn + 1)
        return jnp.bitwise_xor(lax.rem(seq, wide_count), flip) * narrow_count + far

    carry = lax.fori_loop(0, wide_count - 1, take_and_send, carry)
    carry = take(offset_of_arrival(wide_count - 1), carry)
    carry = lax.fori_loop(outside, devices - 1, lambda seq, c: take(offset_of(seq), c), carry)
    real, imag = lax.fori_loop(
        wide_count, outside, lambda seq, c: take(offset_of_arrival(seq), c), carry)
    stats[1, 0] = real
    stats[1, 1] = imag

    @pl.loop(1, devices)
    def _(offset):
        block_copy(offset).wait_send()
        sq_copy(offset).wait()

    def summed(kind):
        totals[kind, 0] = stats[kind]
        total = lax.fori_loop(
            0, devices, lambda device, c: c + totals[kind, jnp.bitwise_xor(me, device)],
            jnp.zeros((2, SUB, LANE), jnp.float32))
        return [jnp.broadcast_to(jnp.sum(total[which]) / amp_total, (SUB, LANE)) for which in range(2)]

    @pl.loop(1, devices)
    def _(offset):
        dot_copy(offset).start()

    mean_first, mean_second = summed(0)
    norms[0] = mean_first[0, 0]
    norms[1] = mean_second[0, 0]
    scale = 1.0 / jnp.sqrt(mean_second + 1e-06)

    piece = part_rows // pieces

    def out_copy(part, at):
        where = pl.ds(pl.multiple_of(part * part_rows + at * piece, piece), piece)
        return pltpu.make_async_copy(outgoing.at[where, :], out_hbm.at[where, :],
                                     out_sem.at[part * pieces + at])

    groups = piece // (SUB * SUB)

    @pl.loop(0, pieces)
    def _(at):
        def group(i, carry):
            base = pl.multiple_of((at * groups + i) * (SUB * SUB), SUB * SUB)
            high = back[SUB + at * groups + i]
            for r in range(SUB):
                start = high + back[r]
                for part in range(2):
                    block = arrived[pl.ds(start + part * (share * SUB), SUB), :]
                    outgoing[pl.ds(base + part * part_rows + r, SUB, stride=SUB), :] = block * scale
            return carry

        lax.fori_loop(0, groups, group, 0, unroll=2)
        for part in range(2):
            out_copy(part, at).start()

    @pl.loop(1, devices)
    def _(offset):
        dot_copy(offset).wait()

    both = jnp.sqrt((mean_first + 1e-06) * (mean_second + 1e-06))
    for which, mean in enumerate(summed(1)):
        intersection[which] = (mean / both)[0, 0]

    @pl.loop(0, pieces)
    def _(at):
        for part in range(2):
            out_copy(part, at).wait()


def local(first_state, second_state, place_first, place_second):
    blocks_dev = first_state.shape[1]
    block = first_state.shape[2]
    wide_count = lax.axis_size("wide")
    narrow_count = lax.axis_size("narrow")
    devices = wide_count * narrow_count
    share = blocks_dev // devices
    lines = 1 + bits(blocks_dev * devices) - bits(LANE)

    def tiles(state):
        split = state.reshape(2, blocks_dev // SUB, SUB, block // LANE, LANE)
        return split.transpose(0, 1, 3, 2, 4).reshape(2 * blocks_dev * SUB, LANE)

    pieces = 8
    rows = (2 * blocks_dev * SUB, LANE)
    any_spec = pl.BlockSpec(memory_space=pl.ANY)
    hbm_spec = pl.BlockSpec(memory_space=pltpu.HBM)
    smem_spec = pl.BlockSpec(memory_space=pltpu.SMEM)
    aligned, intersection, norms = pl.pallas_call(
        functools.partial(exchange, (wide_count, narrow_count), blocks_dev, share, pieces,
                          float(blocks_dev * devices * block)),
        out_shape=(jax.ShapeDtypeStruct(rows, jnp.float32),
                   jax.ShapeDtypeStruct((2,), jnp.float32),
                   jax.ShapeDtypeStruct((2,), jnp.float32)),
        in_specs=[hbm_spec] * 2 + [any_spec] * 2,
        out_specs=(any_spec, smem_spec, smem_spec),
        scratch_shapes=[pltpu.VMEM(rows, jnp.float32)] * 4 + [
            pltpu.VMEM((2, 2, SUB, LANE), jnp.float32),
            pltpu.VMEM((2, devices, 2, SUB, LANE), jnp.float32),
            pltpu.SMEM((2, lines, LANE), jnp.int32),
            pltpu.SMEM((devices + share,), jnp.int32),
            pltpu.SMEM((devices + share,), jnp.int32),
            pltpu.SMEM((SUB + blocks_dev // SUB,), jnp.int32),
            pltpu.SemaphoreType.DMA((2,)),
            pltpu.SemaphoreType.DMA((2 * lines,)),
            pltpu.SemaphoreType.DMA((devices,)),
            pltpu.SemaphoreType.DMA((devices,)),
            pltpu.SemaphoreType.DMA((2 * pieces,)),
        ] + [pltpu.SemaphoreType.DMA((devices,))] * 4,
        compiler_params=pltpu.CompilerParams(
            collective_id=0, has_side_effects=True, vmem_limit_bytes=67043328),
        name="exchange",
    )(place_first.reshape(-1, LANE), place_second.reshape(-1, LANE),
      tiles(first_state), tiles(second_state))
    aligned = aligned.reshape(2, blocks_dev // SUB, block // LANE, SUB, LANE)
    aligned = aligned.transpose(0, 1, 3, 2, 4).reshape(2, blocks_dev, block)
    return (aligned, intersection, norms)


def solution(mesh):
    return jax.shard_map(
        local,
        mesh=mesh,
        in_specs=(P(None, ("wide", "narrow"), None), P(None, ("wide", "narrow"), None), P(), P()),
        out_specs=(P(None, ("wide", "narrow"), None), P(), P()),
        check_vma=False,
    )
```

profile of v0, /device:TPU:0, one launch (start us, length us, event | category | flops | bytes accessed | tf_op | source)
XLA Modules:
  0.0 218.4 jit_solution(18270644120359666547)
XLA Ops:
  0.6 208.2 %exchange.1 = (f32[16384,128]{1,0:T(8,128)}, f32[2]{0:T(128)}, f32[2]{0:T(128)}) custom-call(s32[256,128]{1,0:T(8,128)} %bitcast.20, s32[256,128]{1,0:T(8,128)} %bitcast.21, f32[16384,128]{1,0:T(8,128)} %bitcast.17, f32[16384,128]{1,0:T(8,128)} %bitcast.18), custom_call_target="tpu_custom_call" | custom-call | tf_op jit(solution)/shard_map/exchange/pallas_call | solution.py:310
  208.9 0.0 copy-start.1
  208.9 0.0 copy-start
  208.9 8.4 %copy.10 = f32[2,1024,1024]{2,1,0:T(8,128)} copy(f32[2,1024,1024]{2,1,0:T(8,128)} %bitcast.19) | data formatting | bytes 16777216
  217.3 0.0 copy-done.1
  217.3 0.5 copy.11
  217.8 0.0 copy-done
  217.8 0.5 copy.12
Async XLA Ops:
  208.9 8.5 %copy-start.1 = (f32[2]{0:T(128)S(1)}, f32[2]{0:T(128)}, u32[]{:S(2)}) copy-start(f32[2]{0:T(128)} %get-tuple-element.13) | copy-start | bytes 28
  208.9 9.0 %copy-start = (f32[2]{0:T(128)S(1)}, f32[2]{0:T(128)}, u32[]{:S(2)}) copy-start(f32[2]{0:T(128)} %get-tuple-element.14) | copy-start | bytes 28
where the time goes:
time: 219 us; the launch traced here: 218 us
  Pallas kernels  208 us (95%)
  local copies, waits for them, and re-layouts  9.47 us (4%)
    pallas_call x1, Pallas kernels, local(): pl.pallas_call(functools.partial(exchange, (wide_count, narrow_count), bl...  208 us
    unnamed x7, local copies, waits for them, and re-layouts  9.47 us

commit v1 on v0

v1 whole, which is shorter than its diff:
```python
import functools

import jax
import jax.numpy as jnp
from jax import lax
from jax.experimental import pallas as pl
from jax.experimental.pallas import tpu as pltpu
from jax.sharding import PartitionSpec as P

MESH = pl.DeviceIdType.MESH
SUB = 8
LANE = 128


def row_weight(one_hot):
    return jnp.where(one_hot < SUB, one_hot, one_hot * SUB)


def bits(count):
    return count.bit_length() - 1


def table(ref, base, weights, start=0):
    ref[base] = jnp.int32(start)
    for level, weight in enumerate(weights):
        for low in range(1 << level):
            ref[base + (1 << level) + low] = ref[base + low] + weight


def build_tables(place_f, place_s, blocks_dev, devices, me, share, rows_out, rows_in, back):
    levels = bits(blocks_dev * devices)
    zero = jnp.int32(0)
    dev_out = [zero] * bits(devices)
    dev_in = [zero] * bits(devices)
    k_out = [zero] * bits(share)
    k_in = [zero] * bits(share)
    slot_back = [zero] * bits(blocks_dev)
    unit = jnp.int32(1)
    for level in range(levels):
        f = place_f(level)
        s = place_s(level)
        f_dev = f >> bits(blocks_dev)
        s_dev = s >> bits(blocks_dev)
        both = (f_dev == 0) & (s_dev == 0)
        for j in range(bits(devices)):
            dev_out[j] = dev_out[j] + jnp.where(f_dev == (1 << j), row_weight(s), 0)
            dev_in[j] = dev_in[j] + jnp.where(s_dev == (1 << j), row_weight(f), 0)
        for i in range(bits(share)):
            here = both & (unit == (1 << i))
            k_out[i] = k_out[i] + jnp.where(here, row_weight(s), 0)
            k_in[i] = k_in[i] + jnp.where(here, row_weight(f), 0)
        toward = jnp.where((s_dev & me) == 0, s_dev, -s_dev)
        packed = jnp.where(both, unit * SUB, toward * (2 * share * SUB))
        for p in range(bits(blocks_dev)):
            slot_back[p] = slot_back[p] + jnp.where(f == (1 << p), packed, 0)
        unit = jnp.where(both, unit * 2, unit)
    table(rows_out, 0, dev_out)
    table(rows_out, devices, k_out)
    table(rows_in, 0, dev_in)
    table(rows_in, devices, k_in)
    table(back, 0, slot_back[:bits(SUB)], me * (2 * share * SUB))
    table(back, SUB, slot_back[bits(SUB):])


def exchange(sizes, blocks_dev, share, amp_total, place_first, place_second, first_hbm, second_hbm,
             held, means,
             first, outgoing, arrived, stats, totals, powers, rows_out, rows_in, back,
             load_sem, place_sem, send_sem, recv_sem, sum_send, sum_recv):
    wide_count, narrow_count = sizes
    devices = wide_count * narrow_count
    levels = bits(blocks_dev * devices)
    me_w = lax.axis_index("wide")
    me_n = lax.axis_index("narrow")
    me = me_w * narrow_count + me_n
    part_rows = blocks_dev * SUB
    message = 2 * share * SUB

    lines = [0] + [1 << line for line in range(levels - bits(LANE))]
    fetches = []
    for which, place in enumerate((place_first, place_second)):
        for at, line in enumerate(lines):
            fetches.append(pltpu.make_async_copy(
                place.at[pl.ds(line, 1), :], powers.at[which, pl.ds(at, 1), :],
                place_sem.at[which * len(lines) + at]))
    load_second = pltpu.make_async_copy(second_hbm, held, load_sem.at[0])
    load_first = pltpu.make_async_copy(first_hbm, first, load_sem.at[1])
    for fetch in fetches:
        fetch.start()
    load_second.start()

    def partner(offset):
        return (jnp.bitwise_xor(me_w, offset // narrow_count),
                jnp.bitwise_xor(me_n, lax.rem(offset, narrow_count)))

    def other(offset):
        other_w, other_n = partner(offset)
        return other_w * narrow_count + other_n

    barrier = pltpu.get_barrier_semaphore()

    @pl.loop(1, devices)
    def _(offset):
        pl.semaphore_signal(barrier, inc=1, device_id=partner(offset), device_id_type=MESH)

    for fetch in fetches:
        fetch.wait()

    def place_of(which):
        def entry(level):
            if (1 << level) < LANE:
                return powers[which, 0, 1 << level]
            return powers[which, 1 + level - bits(LANE), 0]
        return entry

    build_tables(place_of(0), place_of(1), blocks_dev, devices, me, share, rows_out, rows_in, back)
    load_second.wait()
    load_first.start()
    pl.semaphore_wait(barrier, devices - 1)

    last = narrow_count - 1
    inner = (me_n != 0) & (me_n != last)
    flip = jnp.where(lax.rem(me_w, 2) == 1, wide_count - 1, 0)

    def offset_of(seq):
        group = seq // narrow_count
        turn = lax.rem(seq, narrow_count)
        far = jnp.where(inner, jnp.where(turn == 0, last, turn), turn + 1)
        away = jnp.bitwise_xor(group, flip) * narrow_count + far
        return jnp.where(turn < last, away, (group + 1) * narrow_count)

    def rows_at(ref, offset):
        return ref.at[pl.ds(pl.multiple_of(offset * message, message), message), :]

    def block_at(offset, part, k):
        return pl.ds(pl.multiple_of(offset * message + (part * share + k) * SUB, SUB), SUB)

    def block_copy(offset):
        return pltpu.make_async_remote_copy(
            src_ref=rows_at(outgoing, offset), dst_ref=rows_at(arrived, offset),
            send_sem=send_sem.at[offset], recv_sem=recv_sem.at[offset],
            device_id=partner(offset), device_id_type=MESH)

    def pack(offset, out):
        base = rows_out[other(offset)]

        def row(k, carry):
            start = base + rows_out[devices + k]
            for part in range(2):
                out[block_at(offset, part, k), :] = held[pl.ds(start + part * part_rows, SUB, stride=SUB), :]
            return carry

        lax.fori_loop(0, share, row, 0, unroll=min(8, share))

    def pack_and_send(seq):
        pack(offset_of(seq), outgoing)
        block_copy(offset_of(seq - 1)).start()

    def sum_copy(kind, offset):
        return pltpu.make_async_remote_copy(
            src_ref=stats.at[kind], dst_ref=totals.at[kind, me],
            send_sem=sum_send.at[kind, offset], recv_sem=sum_recv.at[kind, offset],
            device_id=partner(offset), device_id_type=MESH)

    def keep_sums(kind, sums):
        for which in range(2):
            stats[kind, pl.ds(which, 1), :] = jnp.sum(sums[which], axis=0, keepdims=True)
        totals[kind, me] = stats[kind]

    def send_sums(kind):
        @pl.loop(1, devices)
        def _(offset):
            sum_copy(kind, offset).start()

    def summed(kind):
        @pl.loop(1, devices)
        def _(offset):
            sum_copy(kind, offset).wait()

        total = jnp.sum(totals[kind], axis=0)
        return [jnp.broadcast_to(jnp.sum(total[which:which + 1]) / amp_total, (SUB, LANE)) for which in range(2)]

    early = devices // 2
    pack(offset_of(0), outgoing)
    pl.loop(1, early)(pack_and_send)

    load_first.wait()
    chunk = 16 * SUB

    def squares(i, carry):
        at = pl.multiple_of(i * chunk, chunk)
        a = first[pl.ds(at, chunk), :].reshape(chunk // SUB, SUB, LANE)
        b = held[pl.ds(at, chunk), :].reshape(chunk // SUB, SUB, LANE)
        return carry[0] + jnp.sum(a * a, axis=0), carry[1] + jnp.sum(b * b, axis=0)

    zero = jnp.zeros((SUB, LANE), jnp.float32)
    keep_sums(0, lax.fori_loop(0, 2 * part_rows // chunk, squares, (zero, zero)))
    pack_and_send(early)
    send_sums(0)
    pl.loop(early + 1, devices - 1)(pack_and_send)
    pack(0, arrived)
    block_copy(offset_of(devices - 2)).start()

    def dots(offset, carry):
        base = rows_in[other(offset)]

        def row(k, carry):
            real, imag = carry
            start = base + rows_in[devices + k]
            f_re = first[pl.ds(start, SUB, stride=SUB), :]
            f_im = first[pl.ds(start + part_rows, SUB, stride=SUB), :]
            g_re = arrived[block_at(offset, 0, k), :]
            g_im = arrived[block_at(offset, 1, k), :]
            return real + (f_re * g_re + f_im * g_im), imag + (f_re * g_im - f_im * g_re)

        return lax.fori_loop(0, share, row, carry, unroll=min(8, share))

    def take(seq, carry):
        offset = offset_of(seq)
        block_copy(offset).wait_recv()
        return dots(offset, carry)

    keep_sums(1, lax.fori_loop(0, devices - 1, take, dots(0, (zero, zero))))

    @pl.loop(1, devices)
    def _(offset):
        block_copy(offset).wait_send()

    send_sums(1)
    mean_first, mean_second = summed(0)
    scale = 1.0 / jnp.sqrt(mean_second + 1e-06)

    def group(i, carry):
        base = pl.multiple_of(i * (SUB * SUB), SUB * SUB)
        high = back[SUB + i]
        for r in range(SUB):
            start = high + back[r]
            for part in range(2):
                block = arrived[pl.ds(start + part * (share * SUB), SUB), :]
                held[pl.ds(base + part * part_rows + r, SUB, stride=SUB), :] = block * scale
        return carry

    lax.fori_loop(0, blocks_dev // SUB, group, 0, unroll=2)

    both = jnp.sqrt((mean_first + 1e-06) * (mean_second + 1e-06))
    real, imag = summed(1)
    for row, value in enumerate((real / both, imag / both, mean_first, mean_second)):
        means[pl.ds(row, 1), :] = value[:1]


def store(pieces, held, means, out_hbm, intersection, norms, out_sem):
    piece = held.shape[0] // pieces
    copies = [pltpu.make_async_copy(held.at[pl.ds(at * piece, piece), :], out_hbm.at[pl.ds(at * piece, piece), :],
                                    out_sem.at[at]) for at in range(pieces)]
    for copy in copies:
        copy.start()
    for which in range(2):
        intersection[which] = means[which, 0]
        norms[which] = means[2 + which, 0]
    for copy in copies:
        copy.wait()


def local(first_state, second_state, place_first, place_second):
    blocks_dev = first_state.shape[1]
    block = first_state.shape[2]
    wide_count = lax.axis_size("wide")
    narrow_count = lax.axis_size("narrow")
    devices = wide_count * narrow_count
    share = blocks_dev // devices
    lines = 1 + bits(blocks_dev * devices) - bits(LANE)

    def tiles(state):
        split = state.reshape(2, blocks_dev // SUB, SUB, block // LANE, LANE)
        return split.transpose(0, 1, 3, 2, 4).reshape(2 * blocks_dev * SUB, LANE)

    pieces = 8
    rows = (2 * blocks_dev * SUB, LANE)
    any_spec = pl.BlockSpec(memory_space=pl.ANY)
    hbm_spec = pl.BlockSpec(memory_space=pltpu.HBM)
    vmem_spec = pl.BlockSpec(memory_space=pltpu.VMEM)
    smem_spec = pl.BlockSpec(memory_space=pltpu.SMEM)
    held, means = pl.pallas_call(
        functools.partial(exchange, (wide_count, narrow_count), blocks_dev, share,
                          float(blocks_dev * devices * block)),
        out_shape=(pltpu.VMEM(rows, jnp.float32), pltpu.VMEM((SUB, LANE), jnp.float32)),
        in_specs=[hbm_spec] * 4,
        out_specs=(vmem_spec, vmem_spec),
        scratch_shapes=[pltpu.VMEM(rows, jnp.float32)] * 3 + [
            pltpu.VMEM((2, 2, LANE), jnp.float32),
            pltpu.VMEM((2, devices, 2, LANE), jnp.float32),
            pltpu.SMEM((2, lines, LANE), jnp.int32),
            pltpu.SMEM((devices + share,), jnp.int32),
            pltpu.SMEM((devices + share,), jnp.int32),
            pltpu.SMEM((SUB + blocks_dev // SUB,), jnp.int32),
            pltpu.SemaphoreType.DMA((2,)),
            pltpu.SemaphoreType.DMA((2 * lines,)),
            pltpu.SemaphoreType.DMA((devices,)),
            pltpu.SemaphoreType.DMA((devices,)),
            pltpu.SemaphoreType.DMA((2, devices)),
            pltpu.SemaphoreType.DMA((2, devices)),
        ],
        compiler_params=pltpu.CompilerParams(
            collective_id=0, has_side_effects=True, vmem_limit_bytes=28 << 20),
        name="exchange",
    )(*(pltpu.with_memory_space_constraint(operand, pltpu.HBM) for operand in (
        place_first.reshape(-1, LANE), place_second.reshape(-1, LANE), tiles(first_state), tiles(second_state))))
    aligned, intersection, norms = pl.pallas_call(
        functools.partial(store, pieces),
        out_shape=(jax.ShapeDtypeStruct(rows, jnp.float32),
                   jax.ShapeDtypeStruct((2,), jnp.float32),
                   jax.ShapeDtypeStruct((2,), jnp.float32)),
        in_specs=[vmem_spec] * 2,
        out_specs=(any_spec, smem_spec, smem_spec),
        scratch_shapes=[pltpu.SemaphoreType.DMA((pieces,))],
        compiler_params=pltpu.CompilerParams(vmem_limit_bytes=1 << 20),
        name="store",
    )(held, means)
    aligned = aligned.reshape(2, blocks_dev // SUB, block // LANE, SUB, LANE)
    aligned = aligned.transpose(0, 1, 3, 2, 4).reshape(2, blocks_dev, block)
    return (aligned, intersection, norms)


def solution(mesh):
    return jax.shard_map(
        local,
        mesh=mesh,
        in_specs=(P(None, ("wide", "narrow"), None), P(None, ("wide", "narrow"), None), P(), P()),
        out_specs=(P(None, ("wide", "narrow"), None), P(), P()),
        check_vma=False,
    )
```

time: 219 us -> 207 us (0.945)
  local copies, waits for them, and re-layouts: 9.47 us -> 0 us
    unnamed x7 -> x0, local copies, waits for them, and re-layouts: 9.47 us -> none
    pallas_call x1, Pallas kernels: 208 us -> 202 us  [local(): pl.pallas_call(functools.partial(exchange, (wide_count, narrow_count), bl...]
    pallas_call x0 -> x1, Pallas kernels: none -> 3.89 us  [local(): pl.pallas_call(functools.partial(store, pieces), out_shape=(jax.ShapeDtyp...]
where the time goes in v1:
time: 207 us; the launch traced here: 206 us
  Pallas kernels  206 us (100%)
    pallas_call x1, Pallas kernels, local(): pl.pallas_call(functools.partial(exchange, (wide_count, narrow_count), bl...  202 us

profile of v1, /device:TPU:0, one launch (start us, length us, event | category | flops | bytes accessed | tf_op | source)
XLA Modules:
  0.0 206.4 jit_solution(3928440374828218034)
XLA Ops:
  0.6 201.9 %exchange.1 = (f32[16384,128]{1,0:T(8,128)S(1)}, f32[8,128]{1,0:T(8,128)S(1)}) custom-call(s32[256,128]{1,0:T(8,128)} %bitcast.19, s32[256,128]{1,0:T(8,128)} %bitcast.20, f32[16384,128]{1,0:T(8,128)} %bitcast.17, f32[16384,128]{1,0:T(8,128)} %bitcast.18), custom_call_target="tpu_custom_call" | custom-call | tf_op jit(solution)/shard_map/exchange/pallas_call | solution.py:282
  202.5 3.9 %store.1 = (f32[16384,128]{1,0:T(8,128)}, f32[2]{0:T(128)}, f32[2]{0:T(128)}) custom-call(f32[16384,128]{1,0:T(8,128)S(1)} %get-tuple-element.8.held, f32[8,128]{1,0:T(8,128)S(1)} %get-tuple-element.9.means), custom_call_target="tpu_custom_call" | custom-call | tf_op jit(solution)/shard_map/store/pallas_call | solution.py:307

commit v2 on v1

v2 whole, which is shorter than its diff:
```python
import functools

import jax
import jax.numpy as jnp
from jax import lax
from jax.experimental import pallas as pl
from jax.experimental.pallas import tpu as pltpu
from jax.sharding import PartitionSpec as P

MESH = pl.DeviceIdType.MESH
SUB = 8
LANE = 128


def row_weight(one_hot):
    return jnp.where(one_hot < SUB, one_hot, one_hot * SUB)


def bits(count):
    return count.bit_length() - 1


def table(ref, base, weights, start=0):
    ref[base] = jnp.int32(start)
    for level, weight in enumerate(weights):
        for low in range(1 << level):
            ref[base + (1 << level) + low] = ref[base + low] + weight


def build_tables(place_f, place_s, blocks_dev, devices, me, share, rows_out, rows_in, back):
    levels = bits(blocks_dev * devices)
    zero = jnp.int32(0)
    dev_out = [zero] * bits(devices)
    dev_in = [zero] * bits(devices)
    k_out = [zero] * bits(share)
    k_in = [zero] * bits(share)
    slot_back = [zero] * bits(blocks_dev)
    unit = jnp.int32(1)
    for level in range(levels):
        f = place_f(level)
        s = place_s(level)
        f_dev = f >> bits(blocks_dev)
        s_dev = s >> bits(blocks_dev)
        both = (f_dev == 0) & (s_dev == 0)
        for j in range(bits(devices)):
            dev_out[j] = dev_out[j] + jnp.where(f_dev == (1 << j), row_weight(s), 0)
            dev_in[j] = dev_in[j] + jnp.where(s_dev == (1 << j), row_weight(f), 0)
        for i in range(bits(share)):
            here = both & (unit == (1 << i))
            k_out[i] = k_out[i] + jnp.where(here, row_weight(s), 0)
            k_in[i] = k_in[i] + jnp.where(here, row_weight(f), 0)
        toward = jnp.where((s_dev & me) == 0, s_dev, -s_dev)
        packed = jnp.where(both, unit * SUB, toward * (2 * share * SUB))
        for p in range(bits(blocks_dev)):
            slot_back[p] = slot_back[p] + jnp.where(f == (1 << p), packed, 0)
        unit = jnp.where(both, unit * 2, unit)
    table(rows_out, 0, dev_out)
    table(rows_out, devices, k_out)
    table(rows_in, 0, dev_in)
    table(rows_in, devices, k_in)
    table(back, 0, slot_back[:bits(SUB)], me * (2 * share * SUB))
    table(back, SUB, slot_back[bits(SUB):])


def exchange(sizes, blocks_dev, share, amp_total, place_first, place_second, first_hbm, second_hbm,
             held_re, held_im, sums,
             first, outgoing, arrived, stats, totals, powers, rows_out, rows_in, back,
             load_sem, place_sem, send_sem, recv_sem, sum_send, sum_recv):
    wide_count, narrow_count = sizes
    devices = wide_count * narrow_count
    levels = bits(blocks_dev * devices)
    me_w = lax.axis_index("wide")
    me_n = lax.axis_index("narrow")
    me = me_w * narrow_count + me_n
    part_rows = blocks_dev * SUB
    half = share * SUB
    message = 2 * half
    held = (held_re, held_im)

    def partner(offset):
        return (jnp.bitwise_xor(me_w, offset // narrow_count),
                jnp.bitwise_xor(me_n, lax.rem(offset, narrow_count)))

    def other(offset):
        other_w, other_n = partner(offset)
        return other_w * narrow_count + other_n

    load_second = [pltpu.make_async_copy(second_hbm.at[pl.ds(part * part_rows, part_rows), :], held[part],
                                         load_sem.at[part]) for part in range(2)]
    load_first = pltpu.make_async_copy(first_hbm, first, load_sem.at[2])
    load_second[0].start()
    barrier = pltpu.get_barrier_semaphore()

    @pl.loop(1, devices)
    def _(offset):
        pl.semaphore_signal(barrier, inc=1, device_id=partner(devices - offset), device_id_type=MESH)

    lines = [0] + [1 << line for line in range(levels - bits(LANE))]
    for which, place in enumerate((place_first, place_second)):
        for at, line in enumerate(lines):
            pltpu.make_async_copy(place.at[pl.ds(line, 1), :], powers.at[which, pl.ds(at, 1), :],
                                  place_sem.at[which]).start()
    load_second[1].start()
    for which, place in enumerate((place_first, place_second)):
        pltpu.make_async_copy(place.at[pl.ds(0, len(lines)), :], powers.at[which], place_sem.at[which]).wait()

    def place_of(which):
        def entry(level):
            if (1 << level) < LANE:
                return powers[which, 0, 1 << level]
            return powers[which, 1 + level - bits(LANE), 0]
        return entry

    build_tables(place_of(0), place_of(1), blocks_dev, devices, me, share, rows_out, rows_in, back)

    last = narrow_count - 1
    inner = (me_n != 0) & (me_n != last)
    flip = jnp.where(lax.rem(me_w, 2) == 1, wide_count - 1, 0)

    def offset_of(seq):
        group = seq // narrow_count
        turn = lax.rem(seq, narrow_count)
        far = jnp.where(inner, jnp.where(turn == 0, last, turn), turn + 1)
        away = jnp.bitwise_xor(group, flip) * narrow_count + far
        return jnp.where(turn < last, away, (group + 1) * narrow_count)

    def rows_at(ref, offset):
        return ref.at[pl.ds(pl.multiple_of(offset * message, message), message), :]

    def block_at(offset, part, k):
        return pl.ds(pl.multiple_of(offset * message + (part * share + k) * SUB, SUB), SUB)

    def half_copy(offset, part):
        at = pl.ds(pl.multiple_of(offset * message + part * half, half), half)
        return pltpu.make_async_remote_copy(
            src_ref=outgoing.at[at, :], dst_ref=arrived.at[at, :],
            send_sem=send_sem.at[0], recv_sem=recv_sem.at[offset],
            device_id=partner(offset), device_id_type=MESH)

    def block_copy(offset):
        return pltpu.make_async_remote_copy(
            src_ref=rows_at(outgoing, offset), dst_ref=rows_at(arrived, offset),
            send_sem=send_sem.at[0], recv_sem=recv_sem.at[offset],
            device_id=partner(offset), device_id_type=MESH)

    def pack(offset, out, parts=(0, 1)):
        base = rows_out[other(offset)]

        def row(k, carry):
            start = base + rows_out[devices + k]
            for part in parts:
                out[block_at(offset, part, k), :] = held[part][pl.ds(start, SUB, stride=SUB), :]
            return carry

        lax.fori_loop(0, share, row, 0, unroll=min(8, share))

    def pack_and_send(seq):
        pack(offset_of(seq), outgoing)
        block_copy(offset_of(seq - 1)).start()

    def sum_copy(kind, offset):
        return pltpu.make_async_remote_copy(
            src_ref=stats.at[kind], dst_ref=totals.at[kind, me],
            send_sem=sum_send.at[kind], recv_sem=sum_recv.at[kind],
            device_id=partner(offset), device_id_type=MESH)

    def send_sums(kind, pair):
        for which in range(2):
            stats[kind, pl.ds(which, 1), :] = jnp.sum(pair[which], axis=0, keepdims=True)
        totals[kind, me] = stats[kind]

        @pl.loop(1, devices)
        def _(offset):
            sum_copy(kind, devices - offset).start()

    def summed(kind):
        every = totals.at[kind, pl.ds(0, devices - 1)]
        pltpu.make_async_remote_copy(
            src_ref=every, dst_ref=every, send_sem=sum_send.at[kind], recv_sem=sum_recv.at[kind],
            device_id=partner(1), device_id_type=MESH).wait()
        total = jnp.sum(totals[kind], axis=0)
        sums[pl.ds(2 * kind, 2), :] = total
        return total

    load_second[0].wait()
    pl.semaphore_wait(barrier, devices - 1)
    pack(offset_of(0), outgoing, (0,))
    load_second[1].wait()
    load_first.start()
    half_copy(offset_of(0), 0).start()
    pack(offset_of(0), outgoing, (1,))
    pack(offset_of(1), outgoing)
    half_copy(offset_of(0), 1).start()

    early = devices // 2
    pl.loop(2, early)(pack_and_send)

    load_first.wait()
    chunk = 8 * SUB

    def squares(i, carry):
        at = pl.multiple_of(i * chunk, chunk)
        above = pl.multiple_of(part_rows + i * chunk, chunk)
        ones = [ref[pl.ds(start, chunk), :].reshape(chunk // SUB, SUB, LANE)
                for ref, start in ((first, at), (first, above), (held_re, at), (held_im, at))]
        squared = [jnp.sum(one * one, axis=0) for one in ones]
        return carry[0] + (squared[0] + squared[1]), carry[1] + (squared[2] + squared[3])

    zero = jnp.zeros((SUB, LANE), jnp.float32)
    squared = lax.fori_loop(0, part_rows // chunk, squares, (zero, zero))
    pack_and_send(early)
    send_sums(0, squared)
    pl.loop(early + 1, devices - 1)(pack_and_send)
    pack(0, arrived)
    block_copy(offset_of(devices - 2)).start()

    def dots(offset, carry):
        base = rows_in[other(offset)]

        def row(k, carry):
            real, imag = carry
            start = base + rows_in[devices + k]
            f_re = first[pl.ds(start, SUB, stride=SUB), :]
            f_im = first[pl.ds(start + part_rows, SUB, stride=SUB), :]
            g_re = arrived[block_at(offset, 0, k), :]
            g_im = arrived[block_at(offset, 1, k), :]
            return real + (f_re * g_re + f_im * g_im), imag + (f_re * g_im - f_im * g_re)

        return lax.fori_loop(0, share, row, carry, unroll=min(8, share))

    def arrival_of(seq):
        pair = seq // (2 * narrow_count)
        turn = lax.rem(seq, 2 * narrow_count) // 2
        which = lax.rem(seq, 2)
        far = jnp.where(inner, jnp.where(turn == 1, last, turn - 1), turn)
        mirror = jnp.where(which == 1, wide_count - 1, 0)
        away = jnp.bitwise_xor(2 * pair + lax.rem(me_w, 2), mirror) * narrow_count + far
        return jnp.where(turn == 0, (2 * pair + which) * narrow_count, away)

    def take(seq, carry):
        offset = arrival_of(seq)
        block_copy(offset).wait_recv()
        return dots(offset, carry)

    final = devices - narrow_count
    carry = lax.fori_loop(1, final, take, dots(0, (zero, zero)))
    mean_second = jnp.sum(summed(0)[1:]) / amp_total
    scale = 1.0 / jnp.sqrt(jnp.broadcast_to(mean_second, (SUB, LANE)) + 1e-06)
    send_sums(1, lax.fori_loop(final, devices, take, carry))

    def group(i, carry):
        base = pl.multiple_of(i * (SUB * SUB), SUB * SUB)
        high = back[SUB + i]
        for r in range(SUB):
            start = high + back[r]
            for part in range(2):
                block = arrived[pl.ds(start + part * half, SUB), :]
                held[part][pl.ds(base + r, SUB, stride=SUB), :] = block * scale
        return carry

    lax.fori_loop(0, blocks_dev // SUB, group, 0, unroll=2)
    sent = pl.ds(message, (devices - 1) * message)
    pltpu.make_async_remote_copy(
        src_ref=outgoing.at[sent, :], dst_ref=arrived.at[sent, :],
        send_sem=send_sem.at[0], recv_sem=recv_sem.at[0],
        device_id=partner(1), device_id_type=MESH).wait_send()
    summed(1)


def store(pieces, amp_total, held_re, held_im, sums, out_hbm, intersection_hbm, norms_hbm,
          intersection, norms, out_sem, scalar_sem):
    part_rows = held_re.shape[0]
    piece = part_rows // pieces
    copies = [pltpu.make_async_copy(held.at[pl.ds(at * piece, piece), :],
                                    out_hbm.at[pl.ds(part * part_rows + at * piece, piece), :],
                                    out_sem.at[part * pieces + at])
              for part, held in enumerate((held_re, held_im)) for at in range(pieces)]
    for copy in copies:
        copy.start()
    means = [jnp.broadcast_to(jnp.sum(sums[pl.ds(row, 1), :]) / amp_total, (SUB, LANE)) for row in range(4)]
    both = jnp.sqrt((means[0] + 1e-06) * (means[1] + 1e-06))
    for which in range(2):
        norms[which] = means[which][0, 0]
        intersection[which] = (means[2 + which] / both)[0, 0]
    copies.append(pltpu.make_async_copy(intersection, intersection_hbm, scalar_sem.at[0]))
    copies.append(pltpu.make_async_copy(norms, norms_hbm, scalar_sem.at[1]))
    for copy in copies[-2:]:
        copy.start()
    for copy in copies:
        copy.wait()


def local(first_state, second_state, place_first, place_second):
    blocks_dev = first_state.shape[1]
    block = first_state.shape[2]
    wide_count = lax.axis_size("wide")
    narrow_count = lax.axis_size("narrow")
    devices = wide_count * narrow_count
    share = blocks_dev // devices
    lines = 1 + bits(blocks_dev * devices) - bits(LANE)
    amp_total = float(blocks_dev * devices * block)

    def tiles(state):
        split = state.reshape(2, blocks_dev // SUB, SUB, block // LANE, LANE)
        return split.transpose(0, 1, 3, 2, 4).reshape(2 * blocks_dev * SUB, LANE)

    pieces = 4
    rows = (2 * blocks_dev * SUB, LANE)
    part = (blocks_dev * SUB, LANE)
    any_spec = pl.BlockSpec(memory_space=pl.ANY)
    hbm_spec = pl.BlockSpec(memory_space=pltpu.HBM)
    vmem_spec = pl.BlockSpec(memory_space=pltpu.VMEM)
    held = pl.pallas_call(
        functools.partial(exchange, (wide_count, narrow_count), blocks_dev, share, amp_total),
        out_shape=(pltpu.VMEM(part, jnp.float32), pltpu.VMEM(part, jnp.float32),
                   pltpu.VMEM((SUB, LANE), jnp.float32)),
        in_specs=[hbm_spec] * 4,
        out_specs=(vmem_spec,) * 3,
        scratch_shapes=[pltpu.VMEM(rows, jnp.float32)] * 3 + [
            pltpu.VMEM((2, 2, LANE), jnp.float32),
            pltpu.VMEM((2, devices, 2, LANE), jnp.float32),
            pltpu.SMEM((2, lines, LANE), jnp.int32),
            pltpu.SMEM((devices + share,), jnp.int32),
            pltpu.SMEM((devices + share,), jnp.int32),
            pltpu.SMEM((SUB + blocks_dev // SUB,), jnp.int32),
            pltpu.SemaphoreType.DMA((3,)),
            pltpu.SemaphoreType.DMA((2,)),
            pltpu.SemaphoreType.DMA((1,)),
            pltpu.SemaphoreType.DMA((devices,)),
            pltpu.SemaphoreType.DMA((2,)),
            pltpu.SemaphoreType.DMA((2,)),
        ],
        compiler_params=pltpu.CompilerParams(
            collective_id=0, has_side_effects=True, vmem_limit_bytes=28 << 20),
        name="exchange",
    )(*(pltpu.with_memory_space_constraint(operand, pltpu.HBM) for operand in (
        place_first.reshape(-1, LANE), place_second.reshape(-1, LANE), tiles(first_state), tiles(second_state))))
    aligned, intersection, norms = pl.pallas_call(
        functools.partial(store, pieces, amp_total),
        out_shape=(jax.ShapeDtypeStruct(rows, jnp.float32),
                   jax.ShapeDtypeStruct((2,), jnp.float32),
                   jax.ShapeDtypeStruct((2,), jnp.float32)),
        in_specs=[vmem_spec] * 3,
        out_specs=(any_spec,) * 3,
        scratch_shapes=[
            pltpu.SMEM((2,), jnp.float32),
            pltpu.SMEM((2,), jnp.float32),
            pltpu.SemaphoreType.DMA((2 * pieces,)),
            pltpu.SemaphoreType.DMA((2,)),
        ],
        compiler_params=pltpu.CompilerParams(vmem_limit_bytes=1 << 20),
        name="store",
    )(*held)
    aligned = aligned.reshape(2, blocks_dev // SUB, block // LANE, SUB, LANE)
    aligned = aligned.transpose(0, 1, 3, 2, 4).reshape(2, blocks_dev, block)
    return (aligned, intersection, norms)


def solution(mesh):
    return jax.shard_map(
        local,
        mesh=mesh,
        in_specs=(P(None, ("wide", "narrow"), None), P(None, ("wide", "narrow"), None), P(), P()),
        out_specs=(P(None, ("wide", "narrow"), None), P(), P()),
        check_vma=False,
    )
```

time: 207 us -> 200 us (0.966)
  Pallas kernels: 206 us -> 199 us
    pallas_call x1, Pallas kernels: 202 us -> 195 us  [local(): pl.pallas_call(functools.partial(exchange, (wide_count, narrow_count), bl...]
where the time goes in v2:
time: 200 us; the launch traced here: 199 us
  Pallas kernels  199 us (100%)
    pallas_call x1, Pallas kernels, local(): pl.pallas_call(functools.partial(exchange, (wide_count, narrow_count), bl...  195 us

profile of v2, /device:TPU:0, one launch (start us, length us, event | category | flops | bytes accessed | tf_op | source)
XLA Modules:
  0.0 199.4 jit_solution(16254815419447288257)
XLA Ops:
  0.6 195.3 %exchange.1 = (f32[8192,128]{1,0:T(8,128)S(1)}, f32[8192,128]{1,0:T(8,128)S(1)}, f32[8,128]{1,0:T(8,128)S(1)}) custom-call(s32[256,128]{1,0:T(8,128)} %bitcast.19, s32[256,128]{1,0:T(8,128)} %bitcast.20, f32[16384,128]{1,0:T(8,128)} %bitcast.17, f32[16384,128]{1,0:T(8,128)} %bitcast.18), custom_call_target="tpu_custom_call" | custom-call | tf_op jit(solution)/shard_map/exchange/pallas_call | solution.py:313
  196.0 3.4 %store.1 = (f32[16384,128]{1,0:T(8,128)}, f32[2]{0:T(128)}, f32[2]{0:T(128)}) custom-call(f32[8192,128]{1,0:T(8,128)S(1)} %get-tuple-element.9.held_re, f32[8192,128]{1,0:T(8,128)S(1)} %get-tuple-element.10.held_im, f32[8,128]{1,0:T(8,128)S(1)} %get-tuple-element.11.sums), custom_call_target="tpu_custom_call" | custom-call | tf_op jit(solution)/shard_map/store/pallas_call | solution.py:338

commit v3 on v2

--- a/solution.py
+++ b/solution.py
@@ -27,35 +27,46 @@
             ref[base + (1 << level) + low] = ref[base + low] + weight
 
 
-def build_tables(place_f, place_s, blocks_dev, devices, me, share, rows_out, rows_in, back):
-    levels = bits(blocks_dev * devices)
+def build_out(place_f, place_s, blocks_dev, devices, share, rows_out):
     zero = jnp.int32(0)
     dev_out = [zero] * bits(devices)
+    k_out = [zero] * bits(share)
+    unit = jnp.int32(1)
+    for level in range(bits(blocks_dev * devices)):
+        f = place_f(level)
+        s = place_s(level)
+        f_dev = f >> bits(blocks_dev)
+        both = (f_dev == 0) & ((s >> bits(blocks_dev)) == 0)
+        weight = row_weight(s)
+        for j in range(bits(devices)):
+            dev_out[j] = dev_out[j] + jnp.where(f_dev == (1 << j), weight, 0)
+        for i in range(bits(share)):
+            k_out[i] = k_out[i] + jnp.where(both & (unit == (1 << i)), weight, 0)
+        unit = jnp.where(both, unit * 2, unit)
+    table(rows_out, 0, dev_out)
+    table(rows_out, devices, k_out)
+
+
+def build_in(place_f, place_s, blocks_dev, devices, me, share, rows_in, back):
+    zero = jnp.int32(0)
     dev_in = [zero] * bits(devices)
-    k_out = [zero] * bits(share)
     k_in = [zero] * bits(share)
     slot_back = [zero] * bits(blocks_dev)
     unit = jnp.int32(1)
-    for level in range(levels):
+    for level in range(bits(blocks_dev * devices)):
         f = place_f(level)
-        s = place_s(level)
-        f_dev = f >> bits(blocks_dev)
-        s_dev = s >> bits(blocks_dev)
-        both = (f_dev == 0) & (s_dev == 0)
+        s_dev = place_s(level) >> bits(blocks_dev)
+        both = ((f >> bits(blocks_dev)) == 0) & (s_dev == 0)
+        weight = row_weight(f)
         for j in range(bits(devices)):
-            dev_out[j] = dev_out[j] + jnp.where(f_dev == (1 << j), row_weight(s), 0)
-            dev_in[j] = dev_in[j] + jnp.where(s_dev == (1 << j), row_weight(f), 0)
+            dev_in[j] = dev_in[j] + jnp.where(s_dev == (1 << j), weight, 0)
         for i in range(bits(share)):
-            here = both & (unit == (1 << i))
-            k_out[i] = k_out[i] + jnp.where(here, row_weight(s), 0)
-            k_in[i] = k_in[i] + jnp.where(here, row_weight(f), 0)
+            k_in[i] = k_in[i] + jnp.where(both & (unit == (1 << i)), weight, 0)
         toward = jnp.where((s_dev & me) == 0, s_dev, -s_dev)
         packed = jnp.where(both, unit * SUB, toward * (2 * share * SUB))
         for p in range(bits(blocks_dev)):
             slot_back[p] = slot_back[p] + jnp.where(f == (1 << p), packed, 0)
         unit = jnp.where(both, unit * 2, unit)
-    table(rows_out, 0, dev_out)
-    table(rows_out, devices, k_out)
     table(rows_in, 0, dev_in)
     table(rows_in, devices, k_in)
     table(back, 0, slot_back[:bits(SUB)], me * (2 * share * SUB))
@@ -64,8 +75,8 @@
 
 def exchange(sizes, blocks_dev, share, amp_total, place_first, place_second, first_hbm, second_hbm,
              held_re, held_im, sums,
-             first, outgoing, arrived, stats, totals, powers, rows_out, rows_in, back,
-             load_sem, place_sem, send_sem, recv_sem, sum_send, sum_recv):
+             first, outgoing, arrived, squares, squares_w, squares_n, stats, totals, powers, rows_out, rows_in, back,
+             load_sem, place_sem, send_sem, recv_sem, sum_send, sum_recv, up, down):
     wide_count, narrow_count = sizes
     devices = wide_count * narrow_count
     levels = bits(blocks_dev * devices)
@@ -89,11 +100,19 @@
                                          load_sem.at[part]) for part in range(2)]
     load_first = pltpu.make_async_copy(first_hbm, first, load_sem.at[2])
     load_second[0].start()
+    last = narrow_count - 1
+    inner = (me_n != 0) & (me_n != last)
+    reach = 1 if narrow_count == 4 else last
     barrier = pltpu.get_barrier_semaphore()
-
-    @pl.loop(1, devices)
-    def _(offset):
-        pl.semaphore_signal(barrier, inc=1, device_id=partner(devices - offset), device_id_type=MESH)
+    for plane in reversed(range(narrow_count)):
+        there = jnp.bitwise_xor(me_n, plane)
+
+        @pl.when((there <= me_n + reach) & (there >= me_n - reach))
+        def _():
+            @pl.loop(0, wide_count if plane else wide_count - 1)
+            def _(nearer):
+                offset = (wide_count - 1 - nearer) * narrow_count + plane
+                pl.semaphore_signal(barrier, inc=1, device_id=partner(offset), device_id_type=MESH)
 
     lines = [0] + [1 << line for line in range(levels - bits(LANE))]
     for which, place in enumerate((place_first, place_second)):
@@ -111,16 +130,18 @@
             return powers[which, 1 + level - bits(LANE), 0]
         return entry
 
-    build_tables(place_of(0), place_of(1), blocks_dev, devices, me, share, rows_out, rows_in, back)
-
-    last = narrow_count - 1
-    inner = (me_n != 0) & (me_n != last)
+    build_out(place_of(0), place_of(1), blocks_dev, devices, share, rows_out)
     flip = jnp.where(lax.rem(me_w, 2) == 1, wide_count - 1, 0)
+
+    def swapped(turn):
+        mate = jnp.bitwise_xor(turn, 1)
+        return jnp.where(mate < last, mate, turn) + 1
 
     def offset_of(seq):
         group = seq // narrow_count
         turn = lax.rem(seq, narrow_count)
-        far = jnp.where(inner, jnp.where(turn == 0, last, turn), turn + 1)
+        opening = last - turn
+        far = jnp.where(inner, jnp.where(group == 0, opening, swapped(turn)), turn + 1)
         away = jnp.bitwise_xor(group, flip) * narrow_count + far
         return jnp.where(turn < last, away, (group + 1) * narrow_count)
 
@@ -158,47 +179,77 @@
         pack(offset_of(seq), outgoing)
         block_copy(offset_of(seq - 1)).start()
 
-    def sum_copy(kind, offset):
+    def sum_copy(at, src, dst, offset):
         return pltpu.make_async_remote_copy(
-            src_ref=stats.at[kind], dst_ref=totals.at[kind, me],
-            send_sem=sum_send.at[kind], recv_sem=sum_recv.at[kind],
+            src_ref=src, dst_ref=dst, send_sem=sum_send.at[at], recv_sem=sum_recv.at[at],
             device_id=partner(offset), device_id_type=MESH)
 
-    def send_sums(kind, pair):
+    def keep(ref, pair):
         for which in range(2):
-            stats[kind, pl.ds(which, 1), :] = jnp.sum(pair[which], axis=0, keepdims=True)
-        totals[kind, me] = stats[kind]
-
-        @pl.loop(1, devices)
-        def _(offset):
-            sum_copy(kind, devices - offset).start()
-
-    def summed(kind):
-        every = totals.at[kind, pl.ds(0, devices - 1)]
-        pltpu.make_async_remote_copy(
-            src_ref=every, dst_ref=every, send_sem=sum_send.at[kind], recv_sem=sum_recv.at[kind],
-            device_id=partner(1), device_id_type=MESH).wait()
-        total = jnp.sum(totals[kind], axis=0)
-        sums[pl.ds(2 * kind, 2), :] = total
-        return total
+            ref[pl.ds(which, 1), :] = jnp.sum(pair[which], axis=0, keepdims=True)
+
+    def wait_sums(at, ref):
+        every = ref.at[pl.ds(0, ref.shape[0] - 1)]
+        sum_copy(at, every, every, 1).wait()
+        return jnp.sum(ref[...], axis=0)
+
+    def squares_along_wide(pair):
+        keep(squares, pair)
+        squares_w[me_w] = squares[...]
+
+        @pl.loop(1, wide_count)
+        def _(away):
+            sum_copy(0, squares, squares_w.at[me_w], away * narrow_count).start()
+
+    def squares_along_narrow():
+        total = wait_sums(0, squares_w)
+        squares[...] = total
+        squares_n[me_n] = squares[...]
+
+        @pl.loop(1, narrow_count)
+        def _(plane):
+            sum_copy(1, squares, squares_n.at[me_n], plane).start()
+
+    def send_sums(pair):
+        keep(stats, pair)
+        totals[me] = stats[...]
+
+        for offset in reversed(range(1, devices)):
+            sum_copy(2, stats, totals.at[me], offset).start()
 
     load_second[0].wait()
-    pl.semaphore_wait(barrier, devices - 1)
+    planes = jnp.minimum(me_n + reach, last) - jnp.maximum(me_n - reach, 0) + 1
+    pl.semaphore_wait(barrier, planes * wide_count - 1)
     pack(offset_of(0), outgoing, (0,))
+    half_copy(offset_of(0), 0).start()
     load_second[1].wait()
     load_first.start()
-    half_copy(offset_of(0), 0).start()
     pack(offset_of(0), outgoing, (1,))
+    half_copy(offset_of(0), 1).start()
+    if reach < last:
+        above = me_n < last - 1
+        below = me_n > 1
+
+        def tell(sem, step):
+            pl.semaphore_signal(sem, inc=1, device_id=(me_w, me_n + step), device_id_type=MESH)
+
+        pl.when(inner & ~below)(lambda: tell(up, 1))
+        pl.when(inner & ~above)(lambda: tell(down, -1))
+        pl.when(above)(lambda: pl.semaphore_wait(down, 1))
+        pl.when(inner & above)(lambda: tell(down, -1))
+        pl.when(below)(lambda: pl.semaphore_wait(up, 1))
+        pl.when(inner & below)(lambda: tell(up, 1))
     pack(offset_of(1), outgoing)
-    half_copy(offset_of(0), 1).start()
-
-    early = devices // 2
+
+    early = 6
+    held_back = devices - 3
     pl.loop(2, early)(pack_and_send)
+    build_in(place_of(0), place_of(1), blocks_dev, devices, me, share, rows_in, back)
 
     load_first.wait()
     chunk = 8 * SUB
 
-    def squares(i, carry):
+    def square(i, carry):
         at = pl.multiple_of(i * chunk, chunk)
         above = pl.multiple_of(part_rows + i * chunk, chunk)
         ones = [ref[pl.ds(start, chunk), :].reshape(chunk // SUB, SUB, LANE)
@@ -207,12 +258,16 @@
         return carry[0] + (squared[0] + squared[1]), carry[1] + (squared[2] + squared[3])
 
     zero = jnp.zeros((SUB, LANE), jnp.float32)
-    squared = lax.fori_loop(0, part_rows // chunk, squares, (zero, zero))
+    squared = lax.fori_loop(0, part_rows // chunk, square, (zero, zero))
     pack_and_send(early)
-    send_sums(0, squared)
-    pl.loop(early + 1, devices - 1)(pack_and_send)
+    squares_along_wide(squared)
+    pl.loop(early + 1, held_back + 1)(pack_and_send)
+
+    @pl.loop(held_back + 1, devices - 1)
+    def _(seq):
+        pack(offset_of(seq), outgoing)
+
     pack(0, arrived)
-    block_copy(offset_of(devices - 2)).start()
 
     def dots(offset, carry):
         base = rows_in[other(offset)]
@@ -232,7 +287,7 @@
         pair = seq // (2 * narrow_count)
         turn = lax.rem(seq, 2 * narrow_count) // 2
         which = lax.rem(seq, 2)
-        far = jnp.where(inner, jnp.where(turn == 1, last, turn - 1), turn)
+        far = jnp.where(inner, turn, swapped(turn - 1))
         mirror = jnp.where(which == 1, wide_count - 1, 0)
         away = jnp.bitwise_xor(2 * pair + lax.rem(me_w, 2), mirror) * narrow_count + far
         return jnp.where(turn == 0, (2 * pair + which) * narrow_count, away)
@@ -242,11 +297,21 @@
         block_copy(offset).wait_recv()
         return dots(offset, carry)
 
+    middle = devices // 2 - narrow_count
     final = devices - narrow_count
-    carry = lax.fori_loop(1, final, take, dots(0, (zero, zero)))
-    mean_second = jnp.sum(summed(0)[1:]) / amp_total
+    carry = lax.fori_loop(1, middle, take, dots(0, (zero, zero)))
+    squares_along_narrow()
+
+    @pl.loop(held_back, devices - 1)
+    def _(seq):
+        block_copy(offset_of(seq)).start()
+
+    carry = lax.fori_loop(middle, final, take, carry)
+    total = wait_sums(1, squares_n)
+    sums[pl.ds(0, 2), :] = total
+    mean_second = jnp.sum(total[1:]) / amp_total
     scale = 1.0 / jnp.sqrt(jnp.broadcast_to(mean_second, (SUB, LANE)) + 1e-06)
-    send_sums(1, lax.fori_loop(final, devices, take, carry))
+    send_sums(lax.fori_loop(final, devices, take, carry))
 
     def group(i, carry):
         base = pl.multiple_of(i * (SUB * SUB), SUB * SUB)
@@ -264,7 +329,7 @@
         src_ref=outgoing.at[sent, :], dst_ref=arrived.at[sent, :],
         send_sem=send_sem.at[0], recv_sem=recv_sem.at[0],
         device_id=partner(1), device_id_type=MESH).wait_send()
-    summed(1)
+    sums[pl.ds(2, 2), :] = wait_sums(2, totals)
 
 
 def store(pieces, amp_total, held_re, held_im, sums, out_hbm, intersection_hbm, norms_hbm,
@@ -317,8 +382,11 @@
         in_specs=[hbm_spec] * 4,
         out_specs=(vmem_spec,) * 3,
         scratch_shapes=[pltpu.VMEM(rows, jnp.float32)] * 3 + [
-            pltpu.VMEM((2, 2, LANE), jnp.float32),
-            pltpu.VMEM((2, devices, 2, LANE), jnp.float32),
+            pltpu.VMEM((2, LANE), jnp.float32),
+            pltpu.VMEM((wide_count, 2, LANE), jnp.float32),
+            pltpu.VMEM((narrow_count, 2, LANE), jnp.float32),
+            pltpu.VMEM((2, LANE), jnp.float32),
+            pltpu.VMEM((devices, 2, LANE), jnp.float32),
             pltpu.SMEM((2, lines, LANE), jnp.int32),
             pltpu.SMEM((devices + share,), jnp.int32),
             pltpu.SMEM((devices + share,), jnp.int32),
@@ -327,8 +395,10 @@
             pltpu.SemaphoreType.DMA((2,)),
             pltpu.SemaphoreType.DMA((1,)),
             pltpu.SemaphoreType.DMA((devices,)),
-            pltpu.SemaphoreType.DMA((2,)),
-            pltpu.SemaphoreType.DMA((2,)),
+            pltpu.SemaphoreType.DMA((3,)),
+            pltpu.SemaphoreType.DMA((3,)),
+            pltpu.SemaphoreType.REGULAR,
+            pltpu.SemaphoreType.REGULAR,
         ],
         compiler_params=pltpu.CompilerParams(
             collective_id=0, has_side_effects=True, vmem_limit_bytes=28 << 20),

time: 200 us -> 197 us (0.985)
  Pallas kernels: 199 us -> 196 us
    pallas_call x1, Pallas kernels: 195 us -> 193 us  [local(): pl.pallas_call(functools.partial(exchange, (wide_count, narrow_count), bl...]
where the time goes in v3:
time: 197 us
  Pallas kernels  196 us (99%)
    pallas_call x1, Pallas kernels, local(): pl.pallas_call(functools.partial(exchange, (wide_count, narrow_count), bl...  193 us

profile of v3, /device:TPU:0, one launch (start us, length us, event | category | flops | bytes accessed | tf_op | source)
XLA Modules:
  0.0 196.8 jit_solution(17900802753486005776)
XLA Ops:
  0.6 192.8 %exchange.1 = (f32[8192,128]{1,0:T(8,128)S(1)}, f32[8192,128]{1,0:T(8,128)S(1)}, f32[8,128]{1,0:T(8,128)S(1)}) custom-call(s32[256,128]{1,0:T(8,128)} %bitcast.19, s32[256,128]{1,0:T(8,128)} %bitcast.20, f32[16384,128]{1,0:T(8,128)} %bitcast.17, f32[16384,128]{1,0:T(8,128)} %bitcast.18), custom_call_target="tpu_custom_call" | custom-call | tf_op jit(solution)/shard_map/exchange/pallas_call | solution.py:378
  193.4 3.4 %store.1 = (f32[16384,128]{1,0:T(8,128)}, f32[2]{0:T(128)}, f32[2]{0:T(128)}) custom-call(f32[8192,128]{1,0:T(8,128)S(1)} %get-tuple-element.9.held_re, f32[8192,128]{1,0:T(8,128)S(1)} %get-tuple-element.10.held_im, f32[8,128]{1,0:T(8,128)S(1)} %get-tuple-element.11.sums), custom_call_target="tpu_custom_call" | custom-call | tf_op jit(solution)/shard_map/store/pallas_call | solution.py:408

commit v4 on v3

--- a/solution.py
+++ b/solution.py
@@ -75,7 +75,7 @@
 
 def exchange(sizes, blocks_dev, share, amp_total, place_first, place_second, first_hbm, second_hbm,
              held_re, held_im, sums,
-             first, outgoing, arrived, squares, squares_w, squares_n, stats, totals, powers, rows_out, rows_in, back,
+             first, outgoing, arrived, ready, squares, squares_w, squares_n, stats, totals, powers, rows_out, rows_in, back,
              load_sem, place_sem, send_sem, recv_sem, sum_send, sum_recv, up, down):
     wide_count, narrow_count = sizes
     devices = wide_count * narrow_count
@@ -211,7 +211,9 @@
             sum_copy(1, squares, squares_n.at[me_n], plane).start()
 
     def send_sums(pair):
-        keep(stats, pair)
+        folded = [one + pltpu.roll(one, LANE // 2, 1) for one in pair]
+        lane = lax.broadcasted_iota(jnp.int32, (SUB, LANE), 1)
+        stats[...] = jnp.sum(jnp.where(lane < LANE // 2, folded[0], folded[1]), axis=0, keepdims=True)
         totals[me] = stats[...]
 
         for offset in reversed(range(1, devices)):
@@ -283,6 +285,26 @@
 
         return lax.fori_loop(0, share, row, carry, unroll=min(8, share))
 
+    def dots_ready(slot, offset, carry):
+        def row(k, carry):
+            real, imag = carry
+            f_re, f_im = (ready[block_at(slot, part, k), :] for part in range(2))
+            g_re, g_im = (arrived[block_at(offset, part, k), :] for part in range(2))
+            return real + (f_re * g_re + f_im * g_im), imag + (f_re * g_im - f_im * g_re)
+
+        return lax.fori_loop(0, share, row, carry, unroll=min(16, share))
+
+    def make_ready(seq, slot):
+        base = rows_in[other(arrival_of(seq))]
+
+        def row(k, carry):
+            start = base + rows_in[devices + k]
+            for part in range(2):
+                ready[block_at(slot, part, k), :] = first[pl.ds(start + part * part_rows, SUB, stride=SUB), :]
+            return carry
+
+        lax.fori_loop(0, share, row, 0, unroll=min(8, share))
+
     def arrival_of(seq):
         pair = seq // (2 * narrow_count)
         turn = lax.rem(seq, 2 * narrow_count) // 2
@@ -297,6 +319,11 @@
         block_copy(offset).wait_recv()
         return dots(offset, carry)
 
+    def take_ready(seq, carry):
+        offset = arrival_of(seq)
+        block_copy(offset).wait_recv()
+        return dots_ready(seq - final, offset, carry)
+
     middle = devices // 2 - narrow_count
     final = devices - narrow_count
     carry = lax.fori_loop(1, middle, take, dots(0, (zero, zero)))
@@ -305,13 +332,17 @@
     @pl.loop(held_back, devices - 1)
     def _(seq):
         block_copy(offset_of(seq)).start()
+
+    @pl.loop(final, devices)
+    def _(seq):
+        make_ready(seq, seq - final)
 
     carry = lax.fori_loop(middle, final, take, carry)
     total = wait_sums(1, squares_n)
     sums[pl.ds(0, 2), :] = total
     mean_second = jnp.sum(total[1:]) / amp_total
     scale = 1.0 / jnp.sqrt(jnp.broadcast_to(mean_second, (SUB, LANE)) + 1e-06)
-    send_sums(lax.fori_loop(final, devices, take, carry))
+    send_sums(lax.fori_loop(final, devices, take_ready, carry))
 
     def group(i, carry):
         base = pl.multiple_of(i * (SUB * SUB), SUB * SUB)
@@ -329,7 +360,7 @@
         src_ref=outgoing.at[sent, :], dst_ref=arrived.at[sent, :],
         send_sem=send_sem.at[0], recv_sem=recv_sem.at[0],
         device_id=partner(1), device_id_type=MESH).wait_send()
-    sums[pl.ds(2, 2), :] = wait_sums(2, totals)
+    sums[pl.ds(2, 1), :] = wait_sums(2, totals)
 
 
 def store(pieces, amp_total, held_re, held_im, sums, out_hbm, intersection_hbm, norms_hbm,
@@ -342,7 +373,10 @@
               for part, held in enumerate((held_re, held_im)) for at in range(pieces)]
     for copy in copies:
         copy.start()
-    means = [jnp.broadcast_to(jnp.sum(sums[pl.ds(row, 1), :]) / amp_total, (SUB, LANE)) for row in range(4)]
+    low = lax.broadcasted_iota(jnp.int32, (1, LANE), 1) < LANE // 2
+    dots = sums[pl.ds(2, 1), :]
+    parts = (sums[pl.ds(0, 1), :], sums[pl.ds(1, 1), :], jnp.where(low, dots, 0.0), jnp.where(low, 0.0, dots))
+    means = [jnp.broadcast_to(jnp.sum(one) / amp_total, (SUB, LANE)) for one in parts]
     both = jnp.sqrt((means[0] + 1e-06) * (means[1] + 1e-06))
     for which in range(2):
         norms[which] = means[which][0, 0]
@@ -382,11 +416,12 @@
         in_specs=[hbm_spec] * 4,
         out_specs=(vmem_spec,) * 3,
         scratch_shapes=[pltpu.VMEM(rows, jnp.float32)] * 3 + [
+            pltpu.VMEM((narrow_count * 2 * share * SUB, LANE), jnp.float32),
             pltpu.VMEM((2, LANE), jnp.float32),
             pltpu.VMEM((wide_count, 2, LANE), jnp.float32),
             pltpu.VMEM((narrow_count, 2, LANE), jnp.float32),
-            pltpu.VMEM((2, LANE), jnp.float32),
-            pltpu.VMEM((devices, 2, LANE), jnp.float32),
+            pltpu.VMEM((1, LANE), jnp.float32),
+            pltpu.VMEM((devices, 1, LANE), jnp.float32),
             pltpu.SMEM((2, lines, LANE), jnp.int32),
             pltpu.SMEM((devices + share,), jnp.int32),
             pltpu.SMEM((devices + share,), jnp.int32),

time: 197 us -> 197 us (level)
  no operation moved by 1% of the time
where the time goes in v4:
time: 197 us
  Pallas kernels  196 us (99%)
    pallas_call x1, Pallas kernels, local(): pl.pallas_call(functools.partial(exchange, (wide_count, narrow_count), bl...  193 us

profile of v4, /device:TPU:0, one launch (start us, length us, event | category | flops | bytes accessed | tf_op | source)
XLA Modules:
  0.0 196.6 jit_solution(16809188988102937617)
XLA Ops:
  0.6 192.5 %exchange.1 = (f32[8192,128]{1,0:T(8,128)S(1)}, f32[8192,128]{1,0:T(8,128)S(1)}, f32[8,128]{1,0:T(8,128)S(1)}) custom-call(s32[256,128]{1,0:T(8,128)} %bitcast.19, s32[256,128]{1,0:T(8,128)} %bitcast.20, f32[16384,128]{1,0:T(8,128)} %bitcast.17, f32[16384,128]{1,0:T(8,128)} %bitcast.18), custom_call_target="tpu_custom_call" | custom-call | tf_op jit(solution)/shard_map/exchange/pallas_call | solution.py:412
  193.1 3.4 %store.1 = (f32[16384,128]{1,0:T(8,128)}, f32[2]{0:T(128)}, f32[2]{0:T(128)}) custom-call(f32[8192,128]{1,0:T(8,128)S(1)} %get-tuple-element.9.held_re, f32[8192,128]{1,0:T(8,128)S(1)} %get-tuple-element.10.held_im, f32[8,128]{1,0:T(8,128)S(1)} %get-tuple-element.11.sums), custom_call_target="tpu_custom_call" | custom-call | tf_op jit(solution)/shard_map/store/pallas_call | solution.py:443

commit v5 on v4

--- a/solution.py
+++ b/solution.py
@@ -76,7 +76,7 @@
 def exchange(sizes, blocks_dev, share, amp_total, place_first, place_second, first_hbm, second_hbm,
              held_re, held_im, sums,
              first, outgoing, arrived, ready, squares, squares_w, squares_n, stats, totals, powers, rows_out, rows_in, back,
-             load_sem, place_sem, send_sem, recv_sem, sum_send, sum_recv, up, down):
+             load_sem, place_sem, send_sem, recv_sem, sum_send, sum_recv, known):
     wide_count, narrow_count = sizes
     devices = wide_count * narrow_count
     levels = bits(blocks_dev * devices)
@@ -102,17 +102,33 @@
     load_second[0].start()
     last = narrow_count - 1
     inner = (me_n != 0) & (me_n != last)
-    reach = 1 if narrow_count == 4 else last
+    chained = narrow_count == 4
     barrier = pltpu.get_barrier_semaphore()
-    for plane in reversed(range(narrow_count)):
-        there = jnp.bitwise_xor(me_n, plane)
-
-        @pl.when((there <= me_n + reach) & (there >= me_n - reach))
-        def _():
-            @pl.loop(0, wide_count if plane else wide_count - 1)
-            def _(nearer):
-                offset = (wide_count - 1 - nearer) * narrow_count + plane
-                pl.semaphore_signal(barrier, inc=1, device_id=partner(offset), device_id_type=MESH)
+
+    def greet(where_w, where_n):
+        pl.semaphore_signal(barrier, inc=1, device_id=(where_w, where_n), device_id_type=MESH)
+
+    if chained:
+        for step in (-1, 1, 0):
+            there = me_n + step
+
+            @pl.when((there > 0) & (there < last))
+            def _():
+                for mate in ((0, 1) if step else (1,)):
+                    greet(jnp.bitwise_xor(me_w, mate), there)
+
+        for end in (0, last):
+            @pl.loop(1, wide_count)
+            def _(away):
+                greet(jnp.bitwise_xor(me_w, wide_count - away), end)
+
+            pl.when(me_n != end)(lambda: greet(me_w, end))
+    else:
+        @pl.loop(1, devices)
+        def _(offset):
+            greet(*partner(offset))
+
+    greeted = jnp.where(inner, 5, devices - 1) if chained else devices - 1
 
     lines = [0] + [1 << line for line in range(levels - bits(LANE))]
     for which, place in enumerate((place_first, place_second)):
@@ -137,13 +153,20 @@
         mate = jnp.bitwise_xor(turn, 1)
         return jnp.where(mate < last, mate, turn) + 1
 
+    odd = lax.rem(me_w, 2) == 1
+
     def offset_of(seq):
-        group = seq // narrow_count
-        turn = lax.rem(seq, narrow_count)
+        first_far = jnp.where(inner, last, 1)
+        opened = (wide_count - 2) * narrow_count + jnp.where(inner, last - 1, 0)
+        later = seq - jnp.where(seq <= opened, 1, 0)
+        at = jnp.where(odd, later, seq + jnp.where(seq < last, 0, 1))
+        group = at // narrow_count
+        turn = lax.rem(at, narrow_count)
         opening = last - turn
         far = jnp.where(inner, jnp.where(group == 0, opening, swapped(turn)), turn + 1)
         away = jnp.bitwise_xor(group, flip) * narrow_count + far
-        return jnp.where(turn < last, away, (group + 1) * narrow_count)
+        near = (group + jnp.where(odd, 1, 0)) * narrow_count
+        return jnp.where(odd & (seq == 0), narrow_count + first_far, jnp.where(turn < last, away, near))
 
     def rows_at(ref, offset):
         return ref.at[pl.ds(pl.multiple_of(offset * message, message), message), :]
@@ -220,27 +243,20 @@
             sum_copy(2, stats, totals.at[me], offset).start()
 
     load_second[0].wait()
-    planes = jnp.minimum(me_n + reach, last) - jnp.maximum(me_n - reach, 0) + 1
-    pl.semaphore_wait(barrier, planes * wide_count - 1)
+    pl.semaphore_wait(barrier, greeted)
     pack(offset_of(0), outgoing, (0,))
     half_copy(offset_of(0), 0).start()
     load_second[1].wait()
     load_first.start()
     pack(offset_of(0), outgoing, (1,))
     half_copy(offset_of(0), 1).start()
-    if reach < last:
-        above = me_n < last - 1
-        below = me_n > 1
-
-        def tell(sem, step):
-            pl.semaphore_signal(sem, inc=1, device_id=(me_w, me_n + step), device_id_type=MESH)
-
-        pl.when(inner & ~below)(lambda: tell(up, 1))
-        pl.when(inner & ~above)(lambda: tell(down, -1))
-        pl.when(above)(lambda: pl.semaphore_wait(down, 1))
-        pl.when(inner & above)(lambda: tell(down, -1))
-        pl.when(below)(lambda: pl.semaphore_wait(up, 1))
-        pl.when(inner & below)(lambda: tell(up, 1))
+    if chained:
+        pl.when(inner)(lambda: pl.semaphore_wait(known, 1))
+
+        @pl.when(me_n > 1)
+        def _():
+            pl.semaphore_signal(known, inc=1, device_id=(me_w, me_n - 1), device_id_type=MESH)
+
     pack(offset_of(1), outgoing)
 
     early = 6
@@ -433,7 +449,6 @@
             pltpu.SemaphoreType.DMA((3,)),
             pltpu.SemaphoreType.DMA((3,)),
             pltpu.SemaphoreType.REGULAR,
-            pltpu.SemaphoreType.REGULAR,
         ],
         compiler_params=pltpu.CompilerParams(
             collective_id=0, has_side_effects=True, vmem_limit_bytes=28 << 20),

time: 197 us -> 195 us (0.990)
  no operation moved by 1% of the time
where the time goes in v5:
time: 195 us
  Pallas kernels  195 us (100%)
    pallas_call x1, Pallas kernels, local(): pl.pallas_call(functools.partial(exchange, (wide_count, narrow_count), bl...  191 us

profile of v5, /device:TPU:0, one launch (start us, length us, event | category | flops | bytes accessed | tf_op | source)
XLA Modules:
  0.0 195.2 jit_solution(2934698179146883623)
XLA Ops:
  0.6 191.1 %exchange.1 = (f32[8192,128]{1,0:T(8,128)S(1)}, f32[8192,128]{1,0:T(8,128)S(1)}, f32[8,128]{1,0:T(8,128)S(1)}) custom-call(s32[256,128]{1,0:T(8,128)} %bitcast.19, s32[256,128]{1,0:T(8,128)} %bitcast.20, f32[16384,128]{1,0:T(8,128)} %bitcast.17, f32[16384,128]{1,0:T(8,128)} %bitcast.18), custom_call_target="tpu_custom_call" | custom-call | tf_op jit(solution)/shard_map/exchange/pallas_call | solution.py:428
  191.8 3.4 %store.1 = (f32[16384,128]{1,0:T(8,128)}, f32[2]{0:T(128)}, f32[2]{0:T(128)}) custom-call(f32[8192,128]{1,0:T(8,128)S(1)} %get-tuple-element.9.held_re, f32[8192,128]{1,0:T(8,128)S(1)} %get-tuple-element.10.held_im, f32[8,128]{1,0:T(8,128)S(1)} %get-tuple-element.11.sums), custom_call_target="tpu_custom_call" | custom-call | tf_op jit(solution)/shard_map/store/pallas_call | solution.py:458

commit v6 on v5

--- a/solution.py
+++ b/solution.py
@@ -155,16 +155,19 @@
 
     odd = lax.rem(me_w, 2) == 1
 
+    def turned(group):
+        return jnp.bitwise_xor(group, 2 * jnp.bitwise_and(group, 2)) if wide_count >= 8 else group
+
     def offset_of(seq):
         first_far = jnp.where(inner, last, 1)
-        opened = (wide_count - 2) * narrow_count + jnp.where(inner, last - 1, 0)
+        opened = turned(jnp.int32(wide_count - 2)) * narrow_count + jnp.where(inner, last - 1, 0)
         later = seq - jnp.where(seq <= opened, 1, 0)
         at = jnp.where(odd, later, seq + jnp.where(seq < last, 0, 1))
         group = at // narrow_count
         turn = lax.rem(at, narrow_count)
         opening = last - turn
         far = jnp.where(inner, jnp.where(group == 0, opening, swapped(turn)), turn + 1)
-        away = jnp.bitwise_xor(group, flip) * narrow_count + far
+        away = jnp.bitwise_xor(turned(group), flip) * narrow_count + far
         near = (group + jnp.where(odd, 1, 0)) * narrow_count
         return jnp.where(odd & (seq == 0), narrow_count + first_far, jnp.where(turn < last, away, near))
 
@@ -243,8 +246,8 @@
             sum_copy(2, stats, totals.at[me], offset).start()
 
     load_second[0].wait()
+    pack(offset_of(0), outgoing, (0,))
     pl.semaphore_wait(barrier, greeted)
-    pack(offset_of(0), outgoing, (0,))
     half_copy(offset_of(0), 0).start()
     load_second[1].wait()
     load_first.start()
@@ -327,7 +330,7 @@
         which = lax.rem(seq, 2)
         far = jnp.where(inner, turn, swapped(turn - 1))
         mirror = jnp.where(which == 1, wide_count - 1, 0)
-        away = jnp.bitwise_xor(2 * pair + lax.rem(me_w, 2), mirror) * narrow_count + far
+        away = jnp.bitwise_xor(turned(2 * pair + lax.rem(me_w, 2)), mirror) * narrow_count + far
         return jnp.where(turn == 0, (2 * pair + which) * narrow_count, away)
 
     def take(seq, carry):

time: 195 us -> 195 us (level)
  no operation moved by 1% of the time
where the time goes in v6:
time: 195 us
  Pallas kernels  195 us (100%)
    pallas_call x1, Pallas kernels, local(): pl.pallas_call(functools.partial(exchange, (wide_count, narrow_count), bl...  191 us

profile of v6, /device:TPU:0, one launch (start us, length us, event | category | flops | bytes accessed | tf_op | source)
XLA Modules:
  0.0 195.3 jit_solution(18183380780229879062)
XLA Ops:
  0.6 191.3 %exchange.1 = (f32[8192,128]{1,0:T(8,128)S(1)}, f32[8192,128]{1,0:T(8,128)S(1)}, f32[8,128]{1,0:T(8,128)S(1)}) custom-call(s32[256,128]{1,0:T(8,128)} %bitcast.19, s32[256,128]{1,0:T(8,128)} %bitcast.20, f32[16384,128]{1,0:T(8,128)} %bitcast.17, f32[16384,128]{1,0:T(8,128)} %bitcast.18), custom_call_target="tpu_custom_call" | custom-call | tf_op jit(solution)/shard_map/exchange/pallas_call | solution.py:431
  191.9 3.4 %store.1 = (f32[16384,128]{1,0:T(8,128)}, f32[2]{0:T(128)}, f32[2]{0:T(128)}) custom-call(f32[8192,128]{1,0:T(8,128)S(1)} %get-tuple-element.9.held_re, f32[8192,128]{1,0:T(8,128)S(1)} %get-tuple-element.10.held_im, f32[8,128]{1,0:T(8,128)S(1)} %get-tuple-element.11.sums), custom_call_target="tpu_custom_call" | custom-call | tf_op jit(solution)/shard_map/store/pallas_call | solution.py:461
